TPU v7x, 32 devices: a whole 2x2x4 slice. The times are simulated.
32 devices in a mesh: row: 8 (over z, x), col: 4 (over y, core).
Axes of the slice: x: 2, y: 2, z: 4, core: 2. Of those that a mesh axis runs over, the one named last changes fastest.
Arguments:
- ztrail: float32 [4096, 4096], P('row', 'col'), may hold values from -32 to 32
- panels: float32 [4096, 1024], P('row', 'col'), may hold values from -0.1875 to 0.1875
- window_tiles: float32 [3, 512, 512], P(None, 'row'), may hold values from -3 to 3, as said below
Outputs:
- first_column: float32 [4096, 512], P(('row', 'col'))
- second_column: float32 [4096, 512], P(('row', 'col'))
- corner: float32 [3, 512, 512], P(None, 'row', 'col')
Inputs may be any that keep to these rules, and one draw needn't show every extreme that they name: window_tiles[0] and window_tiles[1] are lower triangular with diagonal entries between 1 and 3.
All inputs are finite; a program needn't handle non-finite values.
Results may differ from a plain program's by a relative error of at most 0.00026.
Values sent between devices are 32-bit elements; how exact they have to be, the bound alone decides.
A program may use at most 64 MiB of HBM per device.

v0:
```python
import jax
import jax.numpy as jnp
from jax import lax
from jax.sharding import PartitionSpec as P


def matmul(left_side, right_side):
    return jnp.dot(
        left_side, right_side, precision=lax.Precision.HIGHEST, preferred_element_type=jnp.float32
    )


def inner_rows(left_rows, right_rows):
    return lax.dot_general(
        left_rows,
        right_rows,
        (((0,), (0,)), ((), ())),
        precision=lax.Precision.HIGHEST,
        preferred_element_type=jnp.float32,
    )


def right_solve(right_side, lower_tile):
    return lax.linalg.triangular_solve(lower_tile, right_side, left_side=False, lower=True)


def left_solve_t(right_side, lower_tile):
    return lax.linalg.triangular_solve(
        lower_tile, right_side, left_side=True, lower=True, transpose_a=True
    )


def corner_share(pivot_first, pivot_second, coupling, gram_aa, gram_ab, gram_bb, unit_share):
    identity = jnp.eye(pivot_first.shape[0], dtype=jnp.float32) * unit_share
    tile_aa = left_solve_t(right_solve(identity + gram_aa, pivot_first), pivot_first)
    weighed = left_solve_t(gram_ab, pivot_first)
    tile_ab = -right_solve(matmul(tile_aa, coupling) - weighed, pivot_second)
    inner = left_solve_t(identity + gram_bb - inner_rows(coupling, weighed), pivot_second)
    tile_bb = right_solve(inner - inner_rows(tile_ab, coupling), pivot_second)
    return jnp.stack([tile_aa, tile_ab, tile_bb], axis=0)


def gram_parts(left_rows, right_rows):
    tile_width = left_rows.shape[1] // 2
    return (
        inner_rows(left_rows[:, :tile_width], right_rows[:, :tile_width]),
        inner_rows(left_rows[:, :tile_width], right_rows[:, tile_width:]),
        inner_rows(left_rows[:, tile_width:], right_rows[:, tile_width:]),
    )


def local(ztrail, panels, window_tiles):
    window = lax.all_gather(window_tiles, "row", axis=1, tiled=True)
    pivot_first = window[0]
    pivot_second = window[1]
    coupling = window[2]
    tile_width = pivot_first.shape[0]
    row_total = lax.axis_size("row")
    col_total = lax.axis_size("col")
    col_index = lax.axis_index("col")
    every_row = lax.all_gather(panels, "row", axis=0, tiled=True)
    far_rows = lax.all_to_all(every_row, "col", split_axis=0, concat_axis=1, tiled=True)
    own_rows = lax.all_gather(panels, "col", axis=1, tiled=True)
    images = lax.psum_scatter(matmul(ztrail, far_rows), "col", scatter_dimension=0, tiled=True)
    row_images = lax.all_gather(images, "col", axis=0, tiled=True)
    gram_aa, gram_ab, gram_bb = gram_parts(own_rows, row_images)
    partial_corner = corner_share(
        pivot_first, pivot_second, coupling, gram_aa, gram_ab, gram_bb, 1.0 / row_total
    )
    block_cols = tile_width // col_total
    column_block = lax.dynamic_slice_in_dim(partial_corner, col_index * block_cols, block_cols, 2)
    corner_block = lax.psum_scatter(column_block, "row", scatter_dimension=1, tiled=True)
    first_column = -right_solve(images[:, :tile_width], pivot_first)
    second_column = -right_solve(
        images[:, tile_width:] + matmul(first_column, coupling), pivot_second
    )
    return (first_column, second_column, corner_block)


def solution(mesh):
    placed = (P("row", "col"), P("row", "col"), P(None, "row", None))
    return jax.shard_map(
        local,
        mesh=mesh,
        in_specs=placed,
        out_specs=(P(("row", "col"), None), P(("row", "col"), None), P(None, "row", "col")),
        check_vma=False,
    )
```

profile of v0, /device:TPU:0, one launch (start us, length us, event | category | flops | bytes accessed | tf_op | source)
XLA Modules:
  0.0 394.4 jit_solution(755672248287215402)
XLA Ops:
  7.2 0.7 all-gather.7.cloned.1.call-update
  8.0 0.7 all-gather.5.cloned.1.call-update
  8.7 76.9 %all-gather.7.cloned.1.call-done = f32[4096,256]{1,0:T(8,128)} async-done(((f32[512,256]{1,0:T(8,128)}), f32[4096,256]{1,0:T(8,128)}) %all-gather.7.cloned.1.call-update) | async-done | bytes 4194320 | tf_op jit(solution)/shard_map/all_gather | solution.py:61
  85.7 53.8 %all_to_all.19 = f32[4,1024,256]{2,1,0:T(8,128)} all-to-all(f32[4,1024,256]{2,1,0:T(8,128)} %bitcast.191), channel_id=1, replica_groups=mesh['row'=8,'col'=4] {'col'}, dimensions={0} | all-to-all | bytes 8388608 | tf_op jit(solution)/shard_map/all_to_all | solution.py:62
  139.5 5.4 %copy.38 = f32[1024,4,256]{0,2,1:T(8,128)} copy(f32[1024,4,256]{2,0,1:T(8,128)} %bitcast.186) | data formatting | bytes 8388608 | tf_op jit(solution)/shard_map/all_to_all | solution.py:62
  144.9 9.7 %fusion.162 = f32[512,1024]{1,0:T(8,128)} fusion(f32[512,1024]{1,0:T(8,128)S(1)} %copy-done, f32[1024,1024]{0,1:T(8,128)} %bitcast.187), kind=kOutput, calls=%fused_computation.223 | convolution fusion | flops 6442450944 | bytes 8388608 | tf_op jit(solution)/shard_map/dot_general | solution.py:8
  155.3 2.8 fusion.3
  158.1 11.3 %while.16 = (s32[]{:T(128)}, f32[512,512]{1,0:T(8,128)}, s32[4,2]{0,1:T(2,128)S(1)}, f32[4,128,128]{2,1,0:T(8,128)S(1)}, s32[]{:T(128)}) while((s32[]{:T(128)}, f32[512,512]{1,0:T(8,128)}, s32[4,2]{0,1:T(2,128)S(1)}, f32[4,128,128]{2,1,0:T(8,128)S(1)}, s32[]{:T(128)}) %tuple.66), condition=%wide.while_cond, body=%wide.while_body.sunk | while | flops 2 | bytes 131189 | solution.py:24
  158.7 2.2 bitcast_dynamic-update-slice_fusion.4
  161.5 2.2 bitcast_dynamic-update-slice_fusion.4
  164.3 2.2 bitcast_dynamic-update-slice_fusion.4
  167.2 2.2 bitcast_dynamic-update-slice_fusion.4
  169.3 39.9 %custom-call.14 = f32[4,128,128]{1,2,0:T(8,128)} custom-call(f32[4,128,128]{2,1,0:T(8,128)S(1)} %get-tuple-element.60), custom_call_target="InvertDiagBlocksLowerTriangular" | custom-call | tf_op jit(solution)/shard_map/triangular_solve/custom-call.1 | solution.py:24
  209.4 7.7 %while.17 = (s32[]{:T(128)}, f32[512,512]{1,0:T(8,128)S(1)}, s32[4,2]{0,1:T(2,128)S(1)}, f32[4,128,128]{2,1,0:T(8,128)S(1)}, s32[]{:T(128)}) while((s32[]{:T(128)}, f32[512,512]{1,0:T(8,128)S(1)}, s32[4,2]{0,1:T(2,128)S(1)}, f32[4,128,128]{2,1,0:T(8,128)S(1)}, s32[]{:T(128)}) %tuple.84), condition=%wide.while_cond.clone, body=%wide.while_body.clone.sunk | while | flops 2 | bytes 131189 | solution.py:24
  210.0 1.3 bitcast_dynamic-update-slice_fusion.5
  211.9 1.3 bitcast_dynamic-update-slice_fusion.5
  213.8 1.3 bitcast_dynamic-update-slice_fusion.5
  215.7 1.3 bitcast_dynamic-update-slice_fusion.5
  217.1 0.7 copy-done.37
  217.8 40.6 %custom-call.15 = f32[4,128,128]{1,2,0:T(8,128)S(1)} custom-call(f32[4,128,128]{2,1,0:T(8,128)} %copy-done.37), custom_call_target="InvertDiagBlocksLowerTriangular" | custom-call | tf_op jit(solution)/shard_map/triangular_solve/custom-call.1 | solution.py:24
  258.4 1.2 fusion.107
  259.6 1.2 convolution_subtract_fusion.23
  260.8 1.1 fusion.112
  261.9 1.3 convolution_subtract_fusion.22
  263.2 1.1 fusion.116
  264.3 1.5 convolution_subtract_fusion.25
  265.8 1.1 fusion.120
  266.9 2.0 convolution_add_fusion
  269.0 0.7 copy-done.29
  269.7 0.9 fusion.105
  270.6 3.5 convolution_bitcast_fusion.2
  275.5 1.0 convolution_subtract_fusion.8
  276.9 1.5 convolution_subtract_fusion.17
  278.8 1.9 select_add_fusion.1
  281.9 0.7 convolution_subtract_fusion.12
  283.0 0.7 convolution_subtract_fusion.19
  284.5 0.6 convolution_subtract_fusion.11
  285.5 1.0 convolution_subtract_fusion.10
  286.9 1.5 convolution_subtract_fusion.18
  288.8 3.2 convolution_subtract_fusion.1
  292.1 1.0 copy-done.30
  293.0 1.9 fusion.65
  295.0 1.8 copy.48
  296.8 1.8 convolution_subtract_fusion.7
  298.5 3.4 select_add_fusion
  302.0 3.1 fusion
  306.5 1.0 convolution_subtract_fusion.4
  307.9 1.5 convolution_subtract_fusion.15
  311.2 0.8 convolution_subtract_fusion.16
  312.4 1.9 convolution_subtract_fusion
  314.3 1.0 copy-done.32
  315.3 1.1 fusion.61
  316.4 1.8 copy.58
  318.2 1.7 convolution_subtract_fusion.3
  319.9 1.3 fusion.42
  322.6 1.1 convolution_subtract_fusion.14
  324.3 1.0 fusion.10
  325.3 1.6 maximum_negate_fusion.2
  326.9 1.8 copy.65
  328.7 1.2 convolution_subtract_fusion.21
  330.2 1.3 convolution_subtract_fusion.20
  331.7 1.4 convolution_subtract_fusion.24
  333.4 0.8 copy.66
  334.2 52.9 %reduce-scatter.5.cloned.1.call-done = f32[3,64,128]{2,1,0:T(8,128)} async-done(((f32[3,512,128]{2,1,0:T(8,128)}), f32[3,64,128]{2,1,0:T(8,128)}) %reduce-scatter.5.cloned.1.call-update) | async-done | bytes 98320 | tf_op jit(solution)/shard_map/reduce_scatter | solution.py:72
  (139 shorter events, 17.9 us)
Async XLA Ops:
  7.2 137.7 %copy-start = (f32[512,1024]{1,0:T(8,128)S(1)}, f32[512,1024]{1,0:T(8,128)}, u32[]{:S(2)}) copy-start(f32[512,1024]{1,0:T(8,128)} %param.9) | copy-start | bytes 6291460
  7.2 78.5 %all-gather.7.cloned.1.call-start = ((), (), s32[]{:S(2)}) async-start(), calls=%async_computation.4 | async-start | bytes 4718592 | tf_op jit(solution)/shard_map/all_gather | solution.py:61
  7.9 147.3 %all-gather.5.cloned.1.call-start = ((), (), s32[]{:S(2)}) async-start(), calls=%async_computation.3 | async-start | bytes 3538944 | tf_op jit(solution)/shard_map/all_gather | solution.py:53
  8.7 200.6 %reduce-scatter.3.cloned.1.call-start = ((), (), s32[]{:S(2)}) async-start(), calls=%async_computation.5 | async-start | bytes 2621440 | tf_op jit(solution)/shard_map/reduce_scatter | solution.py:64
  154.6 116.0 %all-gather.11.cloned.1.call-start = ((), (), s32[]{:S(2)}) async-start(), calls=%async_computation.7 | async-start | bytes 2621440 | tf_op jit(solution)/shard_map/all_gather | solution.py:63
  155.2 115.4 %all-gather.9.cloned.1.call-start = ((), (), s32[]{:S(2)}) async-start(), calls=%async_computation.6 | async-start | bytes 2621440 | tf_op jit(solution)/shard_map/all_gather | solution.py:65
  209.3 177.8 %reduce-scatter.5.cloned.1.call-start = ((), (), s32[]{:S(2)}) async-start(), calls=%async_computation.8 | async-start | bytes 884736 | tf_op jit(solution)/shard_map/reduce_scatter | solution.py:72
  217.1 0.7 copy-start.37
  258.4 15.7 %copy-start.7 = (f32[4,128,128]{1,2,0:T(8,128)}, f32[4,128,128]{1,2,0:T(8,128)S(1)}, u32[]{:S(2)}) copy-start(f32[4,128,128]{1,2,0:T(8,128)S(1)} %custom-call.15) | copy-start | bytes 786436
  258.4 8.5 %copy-start.24 = (f32[128,1024]{1,0:T(8,128)S(1)}, f32[128,1024]{1,0:T(8,128)}, u32[]{:S(2)}) copy-start(f32[128,1024]{1,0:T(8,128)} %reduce-scatter.3.cloned.1.call-done) | copy-start | bytes 1572868
  264.3 4.6 %copy-start.34 = (f32[128,128]{0,1:T(8,128)}, f32[128,128]{0,1:T(8,128)S(1)}, u32[]{:S(2)}) copy-start(f32[128,128]{0,1:T(8,128)S(1)} %fusion.116) | copy-start | bytes 196612
  266.9 2.1 copy-start.36
  268.9 0.7 copy-start.29
  270.6 3.5 copy-start.11
  270.6 3.9 copy-start.1
  274.5 14.3 %copy-start.2 = (f32[128,512]{1,0:T(8,128)}, f32[128,512]{1,0:T(8,128)S(1)}, u32[]{:S(2)}) copy-start(f32[128,512]{1,0:T(8,128)S(1)} %fusion.67) | copy-start | bytes 786436
  275.1 3.7 copy-start.5
  275.1 3.7 copy-start.6
  275.5 13.3 %copy-start.14 = (f32[128,512]{1,0:T(8,128)}, f32[128,512]{1,0:T(8,128)S(1)}, u32[]{:S(2)}) copy-start(f32[128,512]{1,0:T(8,128)S(1)} %fusion.109) | copy-start | bytes 786436
  276.9 11.9 %copy-start.21 = (f32[128,512]{1,0:T(8,128)}, f32[128,512]{1,0:T(8,128)S(1)}, u32[]{:S(2)}) copy-start(f32[128,512]{1,0:T(8,128)S(1)} %fusion.113) | copy-start | bytes 786436
  278.8 10.0 %copy-start.28 = (f32[128,512]{1,0:T(8,128)}, f32[128,512]{1,0:T(8,128)S(1)}, u32[]{:S(2)}) copy-start(f32[128,512]{1,0:T(8,128)S(1)} %fusion.117) | copy-start | bytes 786436
  285.5 6.5 %copy-start.12 = (f32[128,512]{1,0:T(8,128)}, f32[128,512]{1,0:T(8,128)S(1)}, u32[]{:S(2)}) copy-start(f32[128,512]{1,0:T(8,128)S(1)} %fusion.110) | copy-start | bytes 786436
  286.9 5.1 %copy-start.19 = (f32[128,512]{1,0:T(8,128)}, f32[128,512]{1,0:T(8,128)S(1)}, u32[]{:S(2)}) copy-start(f32[128,512]{1,0:T(8,128)S(1)} %fusion.114) | copy-start | bytes 786436
  288.8 3.2 copy-start.26
  292.0 1.0 copy-start.30
  296.7 5.2 %copy-start.3 = (f32[128,512]{1,0:T(8,128)S(1)}, f32[128,512]{1,0:T(8,128)}, u32[]{:S(2)}) copy-start(f32[128,512]{1,0:T(8,128)} %copy-done.2) | copy-start | bytes 786436
  296.7 5.2 %copy-start.4 = (f32[3,512,512]{2,1,0:T(8,128)S(1)}, f32[3,512,512]{2,1,0:T(8,128)}, u32[]{:S(2)}) copy-start(f32[3,512,512]{2,1,0:T(8,128)} %all-gather.5.cloned.1.call-done) | copy-start | bytes 9437188
  296.7 5.2 %copy-start.15 = (f32[128,512]{1,0:T(8,128)S(1)}, f32[128,512]{1,0:T(8,128)}, u32[]{:S(2)}) copy-start(f32[128,512]{1,0:T(8,128)} %copy-done.14) | copy-start | bytes 786436
  296.7 5.2 %copy-start.22 = (f32[128,512]{1,0:T(8,128)S(1)}, f32[128,512]{1,0:T(8,128)}, u32[]{:S(2)}) copy-start(f32[128,512]{1,0:T(8,128)} %copy-done.21) | copy-start | bytes 786436
  302.0 3.2 copy-start.8
  306.5 3.7 copy-start.17
  306.5 3.7 copy-start.31
  310.1 4.1 %copy-start.18 = (f32[512,128]{1,0:T(8,128)}, f32[512,128]{1,0:T(8,128)S(1)}, u32[]{:S(2)}) copy-start(f32[512,128]{1,0:T(8,128)S(1)} %fusion.123) | copy-start | bytes 786436
  311.1 3.1 copy-start.23
  312.4 1.9 copy-start.35
  314.3 1.0 copy-start.32
  318.2 3.0 copy-start.9
  318.2 3.4 copy-start.16
  318.2 3.4 copy-start.33
  321.2 2.9 copy-start.13
  321.2 2.9 copy-start.20
  321.2 2.9 copy-start.27
  324.3 5.6 %copy-start.10 = (f32[4,128,128]{1,2,0:T(8,128)S(1)}, f32[4,128,128]{1,2,0:T(8,128)}, u32[]{:S(2)}) copy-start(f32[4,128,128]{1,2,0:T(8,128)} %copy-done.7) | copy-start | bytes 786436
  326.9 6.4 %copy-start.25 = (f32[128,128]{1,0:T(8,128)S(1)}, f32[128,128]{1,0:T(8,128)}, u32[]{:S(2)}) copy-start(f32[128,128]{1,0:T(8,128)} %fusion.105) | copy-start | bytes 196612
Sparse Core Ops, SparseCore 0:
  10.1 75.4 all-gather.6
  87.8 58.5 all-gather.4
  154.7 28.8 reduce-scatter.2
  185.0 23.0 all-gather.10
  209.5 22.6 all-gather.8
  325.5 61.5 reduce-scatter.4
where the time goes:
time: 402 us; the launch traced here: 394 us
  waiting for transfers between devices  132 us (33%)
  other arithmetic  87.4 us (22%)
  matrix products  71.4 us (18%)
  blocking collectives  53.8 us (13%)
  local copies, waits for them, and re-layouts  34 us (8%)
  between operations  15.5 us (4%)
    another operation x5, other arithmetic, right_solve(): lax.linalg.triangular_solve(lower_tile, right_side, left_side=False, lowe...  83.4 us
    all_gather x1, waiting for transfers between devices, local(): every_row = lax.all_gather(panels, 'row', axis=0, tiled=True)  76.9 us
    all_to_all x1, blocking collectives, local(): lax.all_to_all(every_row, 'col', split_axis=0, concat_axis=1, tiled=True)  53.8 us
    reduce_scatter x1, waiting for transfers between devices, local(): lax.psum_scatter(column_block, 'row', scatter_dimension=1, tiled=True)  52.9 us
    another operation x35, matrix products, right_solve(): lax.linalg.triangular_solve(lower_tile, right_side, left_side=False, lowe...  29.1 us
    another operation x29, local copies, waits for them, and re-layouts, right_solve(): lax.linalg.triangular_solve(lower_tile, right_side, left_side=False, lowe...  22.4 us
    dot_general x3, matrix products, matmul(): jnp.dot(left_side, right_side, precision=lax.Precision.HIGHEST, preferred...  14.9 us
    dot_general x5, matrix products, inner_rows(): lax.dot_general(left_rows, right_rows, (((0,), (0,)), ((), ())), precisio...  13.8 us
  transfers between devices with their start and end apart: 6, of which 2 were waited for; matrix products, arithmetic and copies ran while one was open for 35% of the time, Pallas kernels for 0%

commit v1 on v0

v1 whole, which is shorter than its diff:
```python
import functools

import jax
import jax.numpy as jnp
from jax import lax
from jax.experimental import pallas as pl
from jax.experimental.pallas import tpu as pltpu
from jax.sharding import PartitionSpec as P

HIGHEST = lax.Precision.HIGHEST
HIGH = lax.Precision.HIGH
MESH = pl.DeviceIdType.MESH
VMEM_SPEC = pl.BlockSpec(memory_space=pltpu.VMEM)
VMEM_BYTES = 48 * 1024 * 1024


def dot(left, right, dims=((1,), (0,)), precision=HIGH):
    return lax.dot_general(
        left, right, (dims, ((), ())), precision=precision, preferred_element_type=jnp.float32
    )


def gather_kernel(
    cols, group, halves, p_ref, far_ref, own_ref, zbuf,
    zsend, zrecv, ysend, yrecv, xsend, xrecv, osend, orecv,
):
    rows, width = p_ref.shape
    part = rows // halves
    r = lax.axis_index("row")
    c = lax.axis_index("col")
    g = r // group
    j = r % group
    flat = width % 128 == 0

    def slot(ref, column):
        if flat:
            return ref.at[:, pl.ds(pl.multiple_of(column * width, width), width)]
        return ref.at[column]

    def far_at(jj, column, h):
        return slot(far_ref.at[jj], column).at[pl.ds(h * part, part)]

    barrier = pltpu.get_barrier_semaphore()

    def greet(row, col):
        pl.semaphore_signal(barrier, inc=1, device_id=(row, col), device_id_type=MESH)

    for k in range(1, cols):
        greet(r, (c + k) % cols)
    for k in range(1, group):
        greet(g * group + (j + k) % group, c)
    has_left = g > 0
    has_right = g < cols - 1
    pl.when(has_left)(lambda: greet(r - group, c))
    pl.when(has_right)(lambda: greet(r + group, c))
    edges = has_left.astype(jnp.int32) + has_right.astype(jnp.int32)
    pl.semaphore_wait(barrier, cols - 1 + group - 1 + edges)

    pending = []

    def send(cond, src, dst, ssem, rsem, row, col):
        copy = pltpu.make_async_remote_copy(
            src_ref=src, dst_ref=dst, send_sem=ssem, recv_sem=rsem,
            device_id=(row, col), device_id_type=MESH,
        )
        if cond is None:
            copy.start()
        else:
            pl.when(cond)(copy.start)
        pending.append((cond, copy))

    def await_recv(dst, rsem):
        pltpu.make_async_copy(dst, dst, rsem).wait()

    def spread_x(cond, src, column, h):
        for k in range(1, group):
            jj = (j + k) % group
            send(cond, src, far_at(j, column, h), xsend.at[k, column, h],
                 xrecv.at[j, column, h], g * group + jj, c)

    def deliver(cond, src, gs, h):
        remote = gs != c
        local = gs == c
        if cond is not None:
            remote = jnp.logical_and(cond, remote)
            local = jnp.logical_and(cond, local)
        send(remote, src, far_at(j, c, h), ysend.at[gs, h], yrecv.at[c, h], r, gs)
        spread_x(local, src, c, h)

        def keep():
            far_at(j, c, h)[...] = src[...]

        pl.when(local)(keep)

    def relay_x(step):
        mine = jnp.logical_or(g - step == c, g + step == c)
        for h in range(halves):
            for k in range(1, cols):
                column = (c + k) % cols
                block = far_at(j, column, h)
                pl.when(mine)(functools.partial(await_recv, block, yrecv.at[column, h]))
                spread_x(mine, block, column, h)

    for h in range(halves):
        block = p_ref.at[pl.ds(h * part, part)]
        send(has_right, block, zbuf.at[g, pl.ds(h * part, part)], zsend.at[0, g, h],
             zrecv.at[g, h], r + group, c)
        send(has_left, block, zbuf.at[g, pl.ds(h * part, part)], zsend.at[1, g, h],
             zrecv.at[g, h], r - group, c)
    for h in range(halves):
        deliver(None, p_ref.at[pl.ds(h * part, part)], g, h)
    for step in range(1, cols):
        for h in range(halves):
            for side in range(2):
                gs = g - step if side == 0 else g + step
                there = gs >= 0 if side == 0 else gs < cols
                onward = jnp.logical_and(there, has_right if side == 0 else has_left)
                gs = jnp.clip(gs, 0, cols - 1)
                block = zbuf.at[gs, pl.ds(h * part, part)]
                pl.when(there)(functools.partial(await_recv, block, zrecv.at[gs, h]))
                send(onward, block, block, zsend.at[side, gs, h], zrecv.at[gs, h],
                     r + group if side == 0 else r - group, c)
                deliver(there, block, gs, h)
        if step == 1:
            for k in range(1, cols):
                send(None, p_ref, slot(own_ref, c), osend.at[k], orecv.at[c], r, (c + k) % cols)
            slot(own_ref, c)[...] = p_ref[...]
        relay_x(step - 1)
    relay_x(cols - 1)
    for k in range(1, cols):
        column = (c + k) % cols
        await_recv(slot(own_ref, column), orecv.at[column])
    for k in range(1, group):
        jj = (j + k) % group
        for column in range(cols):
            for h in range(halves):
                await_recv(far_at(jj, column, h), xrecv.at[jj, column, h])
    for cond, copy in pending:
        if cond is None:
            copy.wait_send()
        else:
            pl.when(cond)(copy.wait_send)


def gather_panels(panels, row_total, cols):
    rows, width = panels.shape
    group = row_total // cols
    halves = 2
    flat = width % 128 == 0
    shape = (rows, cols * width) if flat else (cols, rows, width)
    dma = pltpu.SemaphoreType.DMA
    far, own = pl.pallas_call(
        functools.partial(gather_kernel, cols, group, halves),
        out_shape=(
            jax.ShapeDtypeStruct((group,) + shape, jnp.float32),
            jax.ShapeDtypeStruct(shape, jnp.float32),
        ),
        in_specs=[VMEM_SPEC],
        out_specs=(VMEM_SPEC, VMEM_SPEC),
        scratch_shapes=[
            pltpu.VMEM((cols, rows, width), jnp.float32),
            dma((2, cols, halves)),
            dma((cols, halves)),
            dma((cols, halves)),
            dma((cols, halves)),
            dma((group, cols, halves)),
            dma((group, cols, halves)),
            dma((cols,)),
            dma((cols,)),
        ],
        compiler_params=pltpu.CompilerParams(
            collective_id=0, has_side_effects=True, vmem_limit_bytes=VMEM_BYTES
        ),
    )(panels)
    if not flat:
        far = jnp.swapaxes(far, 1, 2)
        own = jnp.swapaxes(own, 0, 1)
    return far.reshape(group * rows, cols * width), own.reshape(rows, cols * width)


def exchange_kernel(axis, total, add, x_ref, out_ref, held, send_sem, recv_sem):
    me = lax.axis_index(axis)
    barrier = pltpu.get_barrier_semaphore()
    for k in range(1, total):
        pl.semaphore_signal(
            barrier, inc=1, device_id={axis: (me + k) % total}, device_id_type=MESH
        )
    pl.semaphore_wait(barrier, total - 1)
    copies = []
    for k in range(1, total):
        to = (me + k) % total
        copy = pltpu.make_async_remote_copy(
            src_ref=x_ref.at[to], dst_ref=held.at[k - 1], send_sem=send_sem.at[k - 1],
            recv_sem=recv_sem.at[k - 1], device_id={axis: to}, device_id_type=MESH,
        )
        copy.start()
        copies.append(copy)
    if add:
        out_ref[...] = x_ref[me]
    else:
        out_ref[me] = x_ref[me]
    for k in range(1, total):
        copies[k - 1].wait_recv()
        if add:
            out_ref[...] += held[k - 1]
        else:
            out_ref[(me + total - k) % total] = held[k - 1]
    for copy in copies:
        copy.wait_send()


def exchange(x, axis, add, collective_id):
    total = x.shape[0]
    out = x.shape[1:] if add else x.shape
    return pl.pallas_call(
        functools.partial(exchange_kernel, axis, total, add),
        out_shape=jax.ShapeDtypeStruct(out, jnp.float32),
        in_specs=[VMEM_SPEC],
        out_specs=VMEM_SPEC,
        scratch_shapes=[
            pltpu.VMEM((total - 1,) + x.shape[1:], jnp.float32),
            pltpu.SemaphoreType.DMA((total - 1,)),
            pltpu.SemaphoreType.DMA((total - 1,)),
        ],
        compiler_params=pltpu.CompilerParams(
            collective_id=collective_id, has_side_effects=True, vmem_limit_bytes=VMEM_BYTES
        ),
    )(x)


def batched(left, right):
    return lax.dot_general(
        left, right, (((2,), (1,)), ((0,), (0,))), precision=HIGHEST,
        preferred_element_type=jnp.float32,
    )


def lower_inverses(tiles):
    count, width, _ = tiles.shape
    base = min(128, width)
    blocks = width // base
    diag = jnp.concatenate(
        [tiles[:, i * base : (i + 1) * base, i * base : (i + 1) * base] for i in range(blocks)], 0
    )
    at_row = lax.broadcasted_iota(jnp.int32, (base, base), 0)
    at_col = lax.broadcasted_iota(jnp.int32, (base, base), 1)
    eye = (at_row == at_col).astype(jnp.float32)
    recip = 1.0 / jnp.sum(diag * eye, axis=2)

    def below(size):
        return jnp.logical_and(at_row // (2 * size) == at_col // (2 * size),
                               jnp.logical_and((at_row // size) % 2 == 1, (at_col // size) % 2 == 0))

    inverse = eye * recip[:, None, :] - jnp.where(below(1), diag, 0.0) * (
        recip[:, :, None] * recip[:, None, :]
    )
    size = 2
    while size < base:
        inverse = inverse - batched(batched(inverse, jnp.where(below(size), diag, 0.0)), inverse)
        size *= 2
    parts = [inverse[i * count : (i + 1) * count] for i in range(blocks)]
    while len(parts) > 1:
        wide = parts[0].shape[1]
        merged = []
        for i in range(0, len(parts), 2):
            low = tiles[:, (i + 1) * wide : (i + 2) * wide, i * wide : (i + 1) * wide]
            corner = -batched(batched(parts[i + 1], low), parts[i])
            top = jnp.concatenate([parts[i], jnp.zeros_like(corner)], 2)
            merged.append(jnp.concatenate([top, jnp.concatenate([corner, parts[i + 1]], 2)], 1))
        parts = merged
    return parts[0]


def local(ztrail, panels, window_tiles):
    window = lax.all_gather(window_tiles, "row", axis=1, tiled=True)
    tile = window.shape[1]
    row_total = lax.axis_size("row")
    cols = lax.axis_size("col")
    col_index = lax.axis_index("col")
    far_rows, own_rows = gather_panels(panels, row_total, cols)

    inverses = lower_inverses(window[:2])
    inv_a = inverses[0]
    inv_b = inverses[1]
    inv_ab = -dot(dot(inv_a, window[2], precision=HIGHEST), inv_b, precision=HIGHEST)
    second = jnp.concatenate([inv_ab, inv_b], axis=0)

    partial = dot(ztrail, far_rows)
    share = partial.shape[0] // cols
    images = exchange(partial.reshape(cols, share, 2 * tile), "col", True, 1)
    solved_a = dot(images[:, :tile], inv_a)
    solved_b = dot(images, second)

    block = tile // cols
    solved = jnp.stack([solved_a.reshape(share, cols, block), solved_b.reshape(share, cols, block)], 2)
    solved = jnp.swapaxes(solved.reshape(share, cols, 2 * block), 0, 1)
    row_solved = exchange(solved, "col", False, 2).reshape(cols * share, 2 * block)

    def cut(array):
        return lax.dynamic_slice_in_dim(array, col_index * block, block, 1)

    part = 1.0 / row_total
    cut_ab = cut(inv_ab) * part
    inner_a = dot(own_rows[:, :tile], row_solved, ((0,), (0,)))
    inner_a = inner_a + jnp.concatenate([cut(inv_a) * part, cut_ab], 1)
    inner_b = dot(own_rows[:, tile:], row_solved[:, block:], ((0,), (0,))) + cut(inv_b) * part
    tiles_a = dot(inv_a, inner_a, ((0,), (0,)))
    tile_bb = dot(second, jnp.concatenate([inner_a[:, block:], inner_b], 0), ((0,), (0,)))
    corner = jnp.stack([tiles_a[:, :block], tiles_a[:, block:], tile_bb], 0)
    corner = corner.reshape(3, row_total, tile // row_total, block)
    corner_block = exchange(jnp.swapaxes(corner, 0, 1), "row", True, 3)
    return (-solved_a, -solved_b, corner_block)


def solution(mesh):
    placed = (P("row", "col"), P("row", "col"), P(None, "row", None))
    return jax.shard_map(
        local,
        mesh=mesh,
        in_specs=placed,
        out_specs=(P(("row", "col"), None), P(("row", "col"), None), P(None, "row", "col")),
        check_vma=False,
    )
```

time: 402 us -> 216 us (0.54)
  the two profiles are of different devices: /device:TPU:0 before, /device:TPU:11 now
where the time goes in v1:
time: 216 us; the launch traced here: 215 us
  Pallas kernels  160 us (74%)
  matrix products  28.4 us (13%)
  between operations  14.6 us (7%)
  local copies, waits for them, and re-layouts  8.03 us (4%)
  other arithmetic  3.77 us (2%)
    pallas_call x3, Pallas kernels, exchange(): pl.pallas_call(functools.partial(exchange_kernel, axis, total, add), out_...  93.3 us
    pallas_call x1, Pallas kernels, gather_panels(): pl.pallas_call(functools.partial(gather_kernel, cols, group, halves), out...  66.5 us
    dot_general x9, matrix products, dot(): lax.dot_general(left, right, (dims, ((), ())), precision=precision, prefe...  18 us
    dot_general x18, matrix products, batched(): lax.dot_general(left, right, (((2,), (1,)), ((0,), (0,))), precision=HIGH...  10.4 us
  transfers between devices with their start and end apart: 1, of which 0 were waited for; matrix products, arithmetic and copies ran while one was open for 3% of the time, Pallas kernels for 56%

profile of v1, /device:TPU:11, one launch (start us, length us, event | category | flops | bytes accessed | tf_op | source)
XLA Modules:
  0.0 215.3 jit_solution(13554056604416522959)
XLA Ops:
  7.2 0.0 copy-start
  7.2 0.0 all-gather.2.cloned.1.call-start
  7.2 0.7 all-gather.2.cloned.1.call-update
  7.9 0.0 copy-start.3
  7.9 1.0 copy-done.3
  9.0 66.5 %shard_map.58 = (f32[2,512,1024]{2,1,0:T(8,128)}, f32[512,1024]{1,0:T(8,128)S(1)}) custom-call(f32[512,256]{1,0:T(8,128)S(1)} %copy-done.3), custom_call_target="tpu_custom_call" | custom-call | tf_op jit(solution)/shard_map/pallas_call | solution.py:152
  75.5 0.0 copy-start.1
  75.5 1.4 copy-done.1
  76.9 0.0 copy-done
  76.9 5.8 %fusion.132.x_ref = f32[4,128,1024]{2,1,0:T(8,128)S(1)} fusion(f32[4,128,1024]{2,1,0:T(8,128)S(1)} %bitcast.68, f32[1024,1024,1]{1,0,2:T(8,128)} %bitcast.72), kind=kOutput, calls=%fused_computation.260 | convolution fusion | flops 3221225472 | bytes 8388608 | tf_op jit(solution)/shard_map/dot_general | solution.py:18
  82.7 53.5 %shard_map.59 = f32[128,1024]{1,0:T(8,128)S(1)} custom-call(f32[4,128,1024]{2,1,0:T(8,128)S(1)} %fusion.132.x_ref), custom_call_target="tpu_custom_call" | custom-call | tf_op jit(solution)/shard_map/pallas_call | solution.py:215
  136.4 0.2 fusion.92
  136.5 0.4 fusion.91
  136.9 0.0 all-gather.2.cloned.1.call-done
  137.0 1.1 fusion.126
  138.1 0.2 multiply_reduce_fusion
  138.3 0.8 fusion.32
  139.1 0.8 convolution_subtract_fusion.5
  139.9 0.6 fusion.30
  140.6 0.6 convolution_subtract_fusion.4
  141.2 0.6 fusion.28
  141.9 0.6 convolution_subtract_fusion.3
  142.5 0.6 fusion.26
  143.2 0.6 convolution_subtract_fusion.2
  143.8 0.6 fusion.24
  144.5 0.6 convolution_subtract_fusion.1
  145.1 0.0 copy-start.10
  145.2 0.6 fusion.22
  145.8 0.6 convolution_subtract_fusion
  146.5 0.5 copy-done.10
  147.0 0.3 fusion.59
  147.3 0.3 convolution_negate_fusion.3
  147.6 0.3 fusion.57
  147.9 0.3 convolution_negate_fusion.2
  148.2 0.7 fusion.12
  148.9 0.6 convolution_negate_fusion.1
  149.5 0.2 select_maximum_fusion
  149.8 0.0 copy-start.4
  149.8 2.0 fusion.127
  151.8 1.2 fusion.130
  152.9 1.8 fusion.4
  154.8 0.0 copy-done.4
  154.8 1.9 convolution_negate_fusion
  156.7 0.0 copy-start.6
  156.7 0.0 copy-done.8
  156.7 1.5 fusion.131
  158.2 0.1 stack_reshape.7
  158.3 0.3 copy.13
  158.6 0.1 stack_reshape.6
  158.7 0.3 copy.12
  159.0 0.5 pad_maximum_fusion.4
  159.5 0.4 reshape.50
  159.9 0.0 copy-start.2
  159.9 8.1 %shard_map.60 = f32[4,128,256]{2,1,0:T(8,128)S(1)} custom-call(f32[4,128,256]{2,1,0:T(8,128)S(1)} %bitcast.71), custom_call_target="tpu_custom_call" | custom-call | tf_op jit(solution)/shard_map/pallas_call | solution.py:215
  168.1 0.0 copy-start.5
  168.1 1.1 dynamic-slice_multiply_fusion
  169.2 1.0 multiply_bitcast_fusion
  170.2 1.0 fusion.2
  171.2 1.0 fusion.5
  172.3 2.0 fusion.3
  174.3 1.8 fusion
  176.1 0.1 maximum_bitcast_fusion.x_ref
  176.2 31.7 %shard_map.61 = f32[3,64,128]{2,1,0:T(8,128)S(1)} custom-call(f32[8,3,64,128]{3,2,1,0:T(8,128)S(1)} %maximum_bitcast_fusion.x_ref), custom_call_target="tpu_custom_call" | custom-call | tf_op jit(solution)/shard_map/pallas_call | solution.py:215
  207.9 0.6 copy.23
  (26 shorter events, 0.2 us)
Async XLA Ops:
  7.2 69.7 %copy-start = (f32[512,1024]{1,0:T(8,128)S(1)}, f32[512,1024]{1,0:T(8,128)}, u32[]{:S(2)}) copy-start(f32[512,1024]{1,0:T(8,128)} %param.3) | copy-start | bytes 6291460
  7.2 129.8 %all-gather.2.cloned.1.call-start = ((), (), s32[]{:S(2)}) async-start(), calls=%async_computation | async-start | bytes 3538944 | tf_op jit(solution)/shard_map/all_gather | solution.py:275
  7.9 1.0 copy-start.3
  75.5 1.4 copy-start.1
  145.1 1.9 copy-start.10
  149.8 5.0 %copy-start.4 = (f32[2,512,512]{2,1,0:T(8,128)}, f32[2,512,512]{2,1,0:T(8,128)S(1)}, u32[]{:S(2)}) copy-start(f32[2,512,512]{2,1,0:T(8,128)S(1)} %select_maximum_fusion) | copy-start | bytes 6291460
  151.8 4.9 %copy-start.8 = (f32[512,512]{1,0:T(8,128)}, f32[512,512]{1,0:T(8,128)S(1)}, u32[]{:S(2)}) copy-start(f32[512,512]{1,0:T(8,128)S(1)} %get-tuple-element.12) | copy-start | bytes 3145732
  156.7 1.6 copy-start.6
  159.9 10.3 %copy-start.2 = (f32[512,1024]{1,0:T(8,128)S(1)}, f32[512,1024]{1,0:T(8,128)}, u32[]{:S(2)}) copy-start(f32[512,1024]{1,0:T(8,128)} %copy-done.1) | copy-start | bytes 6291460
  168.1 3.2 %copy-start.5 = (f32[2,512,512]{2,1,0:T(8,128)S(1)}, f32[2,512,512]{2,1,0:T(8,128)}, u32[]{:S(2)}) copy-start(f32[2,512,512]{2,1,0:T(8,128)} %copy-done.4) | copy-start | bytes 6291460
  171.2 3.0 %copy-start.7 = (f32[512,512]{1,0:T(8,128)S(1)}, f32[512,512]{1,0:T(8,128)}, u32[]{:S(2)}) copy-start(f32[512,512]{1,0:T(8,128)} %copy-done.6) | copy-start | bytes 3145732
  171.2 3.0 %copy-start.9 = (f32[512,512]{1,0:T(8,128)S(1)}, f32[512,512]{1,0:T(8,128)}, u32[]{:S(2)}) copy-start(f32[512,512]{1,0:T(8,128)} %copy-done.8) | copy-start | bytes 3145732
Sparse Core Ops, SparseCore 0:
  10.2 73.3 all-gather.1

commit v2 on v1

--- a/solution.py
+++ b/solution.py
@@ -21,8 +21,9 @@
 
 
 def gather_kernel(
-    cols, group, halves, p_ref, far_ref, own_ref, zbuf,
-    zsend, zrecv, ysend, yrecv, xsend, xrecv, osend, orecv,
+    cols, group, halves, p_ref, w_ref, far_ref, own_ref, win_ref, zbuf,
+    zsend, zrecv, ysend, yrecv, xsend, xrecv, osend, orecv, ofwd,
+    wzsend, wzrecv, wxsend, wxrecv, wdsend, wdrecv,
 ):
     rows, width = p_ref.shape
     part = rows // halves
@@ -109,6 +110,29 @@
              zrecv.at[g, h], r - group, c)
     for h in range(halves):
         deliver(None, p_ref.at[pl.ds(h * part, part)], g, h)
+
+    parity = c % 2
+    mate = c + 1 - 2 * parity
+    tall = w_ref.shape[1]
+    half_lanes = w_ref.shape[2] // 2
+
+    def lanes(side):
+        return pl.ds(pl.multiple_of(side * half_lanes, half_lanes), half_lanes)
+
+    def win_at(gg, jj, side):
+        start = pl.multiple_of((gg * group + jj) * tall, tall)
+        return win_ref.at[:, pl.ds(start, tall), lanes(side)]
+
+    def spread_win(cond, src, gg):
+        for k in range(1, group):
+            send(cond, src, win_at(gg, j, parity), wxsend.at[k, gg], wxrecv.at[j, gg],
+                 g * group + (j + k) % group, c)
+
+    own_win = w_ref.at[:, :, lanes(parity)]
+    send(has_right, own_win, win_at(g, j, parity), wzsend.at[0, g], wzrecv.at[g], r + group, c)
+    send(has_left, own_win, win_at(g, j, parity), wzsend.at[1, g], wzrecv.at[g], r - group, c)
+    spread_win(None, own_win, g)
+    win_ref[:, pl.ds(pl.multiple_of(r * tall, tall), tall), :] = w_ref[...]
     for step in range(1, cols):
         for h in range(halves):
             for side in range(2):
@@ -122,14 +146,44 @@
                      r + group if side == 0 else r - group, c)
                 deliver(there, block, gs, h)
         if step == 1:
-            for k in range(1, cols):
-                send(None, p_ref, slot(own_ref, c), osend.at[k], orecv.at[c], r, (c + k) % cols)
+            for k in range(0, cols, 2):
+                to = (c + k) % cols if k else mate
+                send(None, p_ref, slot(own_ref, c), osend.at[k], orecv.at[c], r, to)
             slot(own_ref, c)[...] = p_ref[...]
+        for side in range(2):
+            gs = g - step if side == 0 else g + step
+            there = gs >= 0 if side == 0 else gs < cols
+            onward = jnp.logical_and(there, has_right if side == 0 else has_left)
+            gs = jnp.clip(gs, 0, cols - 1)
+            block = win_at(gs, j, parity)
+            pl.when(there)(functools.partial(await_recv, block, wzrecv.at[gs]))
+            send(onward, block, block, wzsend.at[side, gs], wzrecv.at[gs],
+                 r + group if side == 0 else r - group, c)
+            spread_win(there, block, gs)
+            send(there, block, block, wdsend.at[j, gs], wdrecv.at[j, gs], r, mate)
         relay_x(step - 1)
     relay_x(cols - 1)
+    for k in range(2, cols, 2):
+        column = (c + k) % cols
+        block = slot(own_ref, column)
+        await_recv(block, orecv.at[column])
+        send(None, block, block, ofwd.at[column], orecv.at[column], r, mate)
+    for k in range(1, group):
+        jj = (j + k) % group
+        for gg in range(cols):
+            block = win_at(gg, jj, parity)
+            await_recv(block, wxrecv.at[jj, gg])
+            send(None, block, block, wdsend.at[jj, gg], wdrecv.at[jj, gg], r, mate)
+    for k in range(0, cols, 2):
+        column = (mate + k) % cols
+        await_recv(slot(own_ref, column), orecv.at[column])
     for k in range(1, cols):
-        column = (c + k) % cols
-        await_recv(slot(own_ref, column), orecv.at[column])
+        gg = (g + k) % cols
+        await_recv(win_at(gg, j, 1 - parity), wdrecv.at[j, gg])
+    for k in range(1, group):
+        jj = (j + k) % group
+        for gg in range(cols):
+            await_recv(win_at(gg, jj, 1 - parity), wdrecv.at[jj, gg])
     for k in range(1, group):
         jj = (j + k) % group
         for column in range(cols):
@@ -142,21 +196,23 @@
             pl.when(cond)(copy.wait_send)
 
 
-def gather_panels(panels, row_total, cols):
+def gather_all(panels, window, row_total, cols):
     rows, width = panels.shape
+    deep, tall, tile = window.shape
     group = row_total // cols
     halves = 2
     flat = width % 128 == 0
     shape = (rows, cols * width) if flat else (cols, rows, width)
     dma = pltpu.SemaphoreType.DMA
-    far, own = pl.pallas_call(
+    far, own, full = pl.pallas_call(
         functools.partial(gather_kernel, cols, group, halves),
         out_shape=(
             jax.ShapeDtypeStruct((group,) + shape, jnp.float32),
             jax.ShapeDtypeStruct(shape, jnp.float32),
+            jax.ShapeDtypeStruct((deep, row_total * tall, tile), jnp.float32),
         ),
-        in_specs=[VMEM_SPEC],
-        out_specs=(VMEM_SPEC, VMEM_SPEC),
+        in_specs=[VMEM_SPEC, VMEM_SPEC],
+        out_specs=(VMEM_SPEC, VMEM_SPEC, VMEM_SPEC),
         scratch_shapes=[
             pltpu.VMEM((cols, rows, width), jnp.float32),
             dma((2, cols, halves)),
@@ -167,15 +223,22 @@
             dma((group, cols, halves)),
             dma((cols,)),
             dma((cols,)),
+            dma((cols,)),
+            dma((2, cols)),
+            dma((cols,)),
+            dma((group, cols)),
+            dma((group, cols)),
+            dma((group, cols)),
+            dma((group, cols)),
         ],
         compiler_params=pltpu.CompilerParams(
             collective_id=0, has_side_effects=True, vmem_limit_bytes=VMEM_BYTES
         ),
-    )(panels)
+    )(panels, window)
     if not flat:
         far = jnp.swapaxes(far, 1, 2)
         own = jnp.swapaxes(own, 0, 1)
-    return far.reshape(group * rows, cols * width), own.reshape(rows, cols * width)
+    return far.reshape(group * rows, cols * width), own.reshape(rows, cols * width), full
 
 
 def exchange_kernel(axis, total, add, x_ref, out_ref, held, send_sem, recv_sem):
@@ -228,73 +291,181 @@
     )(x)
 
 
-def batched(left, right):
-    return lax.dot_general(
-        left, right, (((2,), (1,)), ((0,), (0,))), precision=HIGHEST,
-        preferred_element_type=jnp.float32,
-    )
-
-
-def lower_inverses(tiles):
-    count, width, _ = tiles.shape
-    base = min(128, width)
-    blocks = width // base
-    diag = jnp.concatenate(
-        [tiles[:, i * base : (i + 1) * base, i * base : (i + 1) * base] for i in range(blocks)], 0
-    )
+def split(array):
+    high = array.astype(jnp.bfloat16)
+    return high, (array - high.astype(jnp.float32)).astype(jnp.bfloat16)
+
+
+def dot_split(left, right):
+    out = jnp.dot(left[0], right[1], preferred_element_type=jnp.float32)
+    out += jnp.dot(left[1], right[0], preferred_element_type=jnp.float32)
+    return out + jnp.dot(left[0], right[0], preferred_element_type=jnp.float32)
+
+
+def exact(left, right):
+    return jnp.dot(left, right, precision=HIGHEST, preferred_element_type=jnp.float32)
+
+
+def diagonal_inverses(tiles):
+    base = tiles[0].shape[0]
     at_row = lax.broadcasted_iota(jnp.int32, (base, base), 0)
     at_col = lax.broadcasted_iota(jnp.int32, (base, base), 1)
-    eye = (at_row == at_col).astype(jnp.float32)
-    recip = 1.0 / jnp.sum(diag * eye, axis=2)
-
-    def below(size):
-        return jnp.logical_and(at_row // (2 * size) == at_col // (2 * size),
-                               jnp.logical_and((at_row // size) % 2 == 1, (at_col // size) % 2 == 0))
-
-    inverse = eye * recip[:, None, :] - jnp.where(below(1), diag, 0.0) * (
-        recip[:, :, None] * recip[:, None, :]
-    )
-    size = 2
-    while size < base:
-        inverse = inverse - batched(batched(inverse, jnp.where(below(size), diag, 0.0)), inverse)
-        size *= 2
-    parts = [inverse[i * count : (i + 1) * count] for i in range(blocks)]
-    while len(parts) > 1:
-        wide = parts[0].shape[1]
-        merged = []
-        for i in range(0, len(parts), 2):
-            low = tiles[:, (i + 1) * wide : (i + 2) * wide, i * wide : (i + 1) * wide]
-            corner = -batched(batched(parts[i + 1], low), parts[i])
-            top = jnp.concatenate([parts[i], jnp.zeros_like(corner)], 2)
-            merged.append(jnp.concatenate([top, jnp.concatenate([corner, parts[i + 1]], 2)], 1))
-        parts = merged
-    return parts[0]
+
+    def below(level):
+        apart = (at_row >> (level + 1)) == (at_col >> (level + 1))
+        return jnp.logical_and(apart, (at_row >> level) > (at_col >> level))
+
+    inverses = []
+    for tile in tiles:
+        diag = jnp.where(at_row == at_col, tile, 0.0)
+        down = 1.0 / jnp.sum(diag, axis=1, keepdims=True)
+        over = 1.0 / jnp.sum(diag, axis=0, keepdims=True)
+        first = jnp.where(below(0), tile, 0.0) * down * over
+        inverses.append(jnp.where(at_row == at_col, down, 0.0) - first)
+    level = 1
+    while (1 << level) < base:
+        mask = below(level)
+        lows = [exact(inv, jnp.where(mask, tile, 0.0)) for inv, tile in zip(inverses, tiles)]
+        inverses = [inv - exact(low, inv) for inv, low in zip(inverses, lows)]
+        level += 1
+    return inverses
+
+
+def images_kernel(
+    cols, z_ref, far_ref, win_ref, solved_ref, inva_ref, second_ref,
+    far_high, far_low, parts, mated, landed, sums, msend, mrecv, ysend, yrecv,
+):
+    c = lax.axis_index("col")
+    parity = c % 2
+    mate = c + 1 - 2 * parity
+    pairs = cols // 2
+    pair = c // 2
+    share = z_ref.shape[0] // cols
+    tile = win_ref.shape[1]
+    barrier = pltpu.get_barrier_semaphore()
+    pl.semaphore_signal(barrier, inc=1, device_id={"col": mate}, device_id_type=MESH)
+    for k in range(1, pairs):
+        to = (c + 2 * k) % cols
+        pl.semaphore_signal(barrier, inc=1, device_id={"col": to}, device_id_type=MESH)
+
+    far_high[...], far_low[...] = split(far_ref[...])
+
+    def partial(column):
+        rows = z_ref[pl.ds(pl.multiple_of(column * share, share), share), :]
+        return dot_split(split(rows), (far_high[...], far_low[...]))
+
+    def to_mate(k, target):
+        copy = pltpu.make_async_remote_copy(
+            src_ref=parts.at[k], dst_ref=mated.at[k], send_sem=msend.at[k], recv_sem=mrecv.at[k],
+            device_id={"col": target}, device_id_type=MESH,
+        )
+        copy.start()
+        return copy
+
+    mates = []
+    crossed = []
+    order = [*range(1, pairs), 0]
+    for place, k in enumerate(order):
+        other = (pair + k) % pairs
+        parts[k] = partial(2 * other + 1 - parity)
+        if place == 0:
+            pl.semaphore_wait(barrier, pairs)
+        mates.append(to_mate(k, mate))
+    for place, k in enumerate(order):
+        other = (pair + k) % pairs
+        mine = partial(2 * other + parity)
+        mates[place].wait_recv()
+        sums[k] = mine + mated[k]
+        if k:
+            copy = pltpu.make_async_remote_copy(
+                src_ref=sums.at[k], dst_ref=landed.at[k], send_sem=ysend.at[k],
+                recv_sem=yrecv.at[k], device_id={"col": 2 * other + parity}, device_id_type=MESH,
+            )
+            copy.start()
+            crossed.append(copy)
+
+    base = min(256, tile)
+    count = tile // base
+    tiles = [
+        win_ref[which, i * base : (i + 1) * base, i * base : (i + 1) * base]
+        for which in range(2)
+        for i in range(count)
+    ]
+    blocks = diagonal_inverses(tiles)
+    second_ref[...] = jnp.zeros_like(second_ref)
+    inva_ref[...] = jnp.zeros_like(inva_ref)
+
+    def place_inverse(which, out_ref, offset):
+        mine = blocks[which * count : (which + 1) * count]
+        for i in range(count):
+            out_ref[offset + i * base : offset + (i + 1) * base, i * base : (i + 1) * base] = mine[i]
+        for i in range(1, count):
+            wide = i * base
+            low = win_ref[which, wide : wide + base, :wide]
+            above = out_ref[offset : offset + wide, :wide]
+            out_ref[offset + wide : offset + wide + base, :wide] = -exact(exact(mine[i], low), above)
+
+    place_inverse(0, inva_ref, 0)
+    place_inverse(1, second_ref, tile)
+    second_ref[:tile, :] = -exact(exact(inva_ref[...], win_ref[2]), second_ref[tile:, :])
+    inv_a = split(inva_ref[...])
+    second = split(second_ref[...])
+
+    total = sums[0]
+    for place in range(pairs - 1):
+        crossed[place].wait_recv()
+        total += landed[order[place]]
+    high, low = split(total)
+    solved_ref[:, :tile] = dot_split((high[:, :tile], low[:, :tile]), inv_a)
+    solved_ref[:, tile:] = dot_split((high, low), second)
+    for copy in mates + crossed:
+        copy.wait_send()
+
+
+def images_and_inverses(ztrail, far_rows, window, cols):
+    share = ztrail.shape[0] // cols
+    depth, wide = far_rows.shape
+    tile = window.shape[1]
+    pairs = cols // 2
+    dma = pltpu.SemaphoreType.DMA
+    return pl.pallas_call(
+        functools.partial(images_kernel, cols),
+        out_shape=(
+            jax.ShapeDtypeStruct((share, wide), jnp.float32),
+            jax.ShapeDtypeStruct((tile, tile), jnp.float32),
+            jax.ShapeDtypeStruct((2 * tile, tile), jnp.float32),
+        ),
+        in_specs=[VMEM_SPEC] * 3,
+        out_specs=(VMEM_SPEC,) * 3,
+        scratch_shapes=[
+            pltpu.VMEM((depth, wide), jnp.bfloat16),
+            pltpu.VMEM((depth, wide), jnp.bfloat16),
+            *[pltpu.VMEM((pairs, share, wide), jnp.float32)] * 4,
+            *[dma((pairs,))] * 4,
+        ],
+        compiler_params=pltpu.CompilerParams(
+            collective_id=1, has_side_effects=True, vmem_limit_bytes=VMEM_BYTES
+        ),
+    )(ztrail, far_rows, window)
 
 
 def local(ztrail, panels, window_tiles):
-    window = lax.all_gather(window_tiles, "row", axis=1, tiled=True)
-    tile = window.shape[1]
     row_total = lax.axis_size("row")
     cols = lax.axis_size("col")
     col_index = lax.axis_index("col")
-    far_rows, own_rows = gather_panels(panels, row_total, cols)
-
-    inverses = lower_inverses(window[:2])
-    inv_a = inverses[0]
-    inv_b = inverses[1]
-    inv_ab = -dot(dot(inv_a, window[2], precision=HIGHEST), inv_b, precision=HIGHEST)
-    second = jnp.concatenate([inv_ab, inv_b], axis=0)
-
-    partial = dot(ztrail, far_rows)
-    share = partial.shape[0] // cols
-    images = exchange(partial.reshape(cols, share, 2 * tile), "col", True, 1)
-    solved_a = dot(images[:, :tile], inv_a)
-    solved_b = dot(images, second)
+    tile = window_tiles.shape[2]
+    far_rows, own_rows, window = gather_all(panels, window_tiles, row_total, cols)
+    share = ztrail.shape[0] // cols
+    solved, inv_a, second = images_and_inverses(ztrail, far_rows, window, cols)
+    inv_ab = second[:tile]
+    inv_b = second[tile:]
+    solved_a = solved[:, :tile]
+    solved_b = solved[:, tile:]
 
     block = tile // cols
-    solved = jnp.stack([solved_a.reshape(share, cols, block), solved_b.reshape(share, cols, block)], 2)
-    solved = jnp.swapaxes(solved.reshape(share, cols, 2 * block), 0, 1)
-    row_solved = exchange(solved, "col", False, 2).reshape(cols * share, 2 * block)
+    pieces = jnp.stack([solved_a.reshape(share, cols, block), solved_b.reshape(share, cols, block)], 2)
+    pieces = jnp.swapaxes(pieces.reshape(share, cols, 2 * block), 0, 1)
+    row_solved = exchange(pieces, "col", False, 2).reshape(cols * share, 2 * block)
 
     def cut(array):
         return lax.dynamic_slice_in_dim(array, col_index * block, block, 1)

time: 216 us -> 174 us (0.81)
  matrix products: 28.4 us -> 7.02 us
  between operations: 14.6 us -> 0.8 us
  Pallas kernels: 160 us -> 148 us
  local copies, waits for them, and re-layouts: 8.03 us -> 11.6 us
    pallas_call x3 -> x2, Pallas kernels: 93.3 us -> 45.8 us  [exchange(): pl.pallas_call(functools.partial(exchange_kernel, axis, total, add), out_...]
    pallas_call x1 -> x2, Pallas kernels: 66.5 us -> 103 us  [the longest x1 61.5 us: gather_all(): pl.pallas_call(functools.partial(gather_kernel, cols, group, halves), out...]
    dot_general x9 -> x4, matrix products: 18 us -> 7.02 us  [dot(): lax.dot_general(left, right, (dims, ((), ())), precision=precision, prefe...]
    dot_general x18 -> x0, matrix products: 10.4 us -> none  [batched(): lax.dot_general(left, right, (((2,), (1,)), ((0,), (0,))), precision=HIGH...]
    unnamed x23 -> x19, local copies, waits for them, and re-layouts: 3.64 us -> 8.01 us
  transfers between devices with their start and end apart: 1 -> 0, of which waited for: 0 -> 0; matrix products, arithmetic and copies ran while one was open for 3% -> 0% of each run, Pallas kernels for 56% -> 0%
where the time goes in v2:
time: 174 us; the launch traced here: 173 us
  Pallas kernels  148 us (85%)
  local copies, waits for them, and re-layouts  11.6 us (7%)
  matrix products  7.02 us (4%)
  other arithmetic  5.39 us (3%)
    pallas_call x1, Pallas kernels, gather_all(): pl.pallas_call(functools.partial(gather_kernel, cols, group, halves), out...  61.5 us
    pallas_call x2, Pallas kernels, exchange(): pl.pallas_call(functools.partial(exchange_kernel, axis, total, add), out_...  45.8 us
    pallas_call x1, Pallas kernels, images_and_inverses(): pl.pallas_call(functools.partial(images_kernel, cols), out_shape=(jax.Sha...  41 us
    unnamed x19, local copies, waits for them, and re-layouts  8.01 us
    dot_general x4, matrix products, dot(): lax.dot_general(left, right, (dims, ((), ())), precision=precision, prefe...  7.02 us

profile of v2, /device:TPU:11, one launch (start us, length us, event | category | flops | bytes accessed | tf_op | source)
XLA Modules:
  0.0 173.1 jit_solution(12965318244301803917)
XLA Ops:
  0.6 0.0 copy-start.7
  0.6 1.0 copy-done.7
  1.7 0.0 copy-start.8
  1.7 1.0 copy-done.8
  2.7 61.5 %shard_map.58 = (f32[2,512,1024]{2,1,0:T(8,128)}, f32[512,1024]{1,0:T(8,128)S(1)}, f32[3,512,512]{2,1,0:T(8,128)S(1)}) custom-call(f32[512,256]{1,0:T(8,128)S(1)} %copy-done.7, f32[3,64,512]{2,1,0:T(8,128)S(1)} %copy-done.8), custom_call_target="tpu_custom_call" | custom-call | tf_op jit(solution)/shard_map/pallas_call | solution.py:207
  64.2 0.0 copy-start
  64.2 1.7 copy-done
  65.9 0.0 copy-start.1
  65.9 1.4 copy-done.1
  67.3 0.0 copy-start.3
  67.3 1.6 copy-done.3
  68.9 41.0 %shard_map.59 = (f32[128,1024]{1,0:T(8,128)S(1)}, f32[512,512]{1,0:T(8,128)S(1)}, f32[1024,512]{1,0:T(8,128)S(1)}) custom-call(f32[512,1024]{1,0:T(8,128)S(1)} %copy-done.3, f32[1024,1024]{1,0:T(8,128)} %bitcast.17, f32[3,512,512]{2,1,0:T(8,128)} %copy-done), custom_call_target="tpu_custom_call" | custom-call | tf_op jit(solution)/shard_map/pallas_call | solution.py:431
  109.9 0.0 copy-start.6
  110.0 0.0 copy-start.4
  110.0 1.6 fusion.8
  111.6 0.0 copy-done.6
  111.6 0.1 copy-done.4
  111.8 1.7 %dynamic-slice_multiply_fusion = (f32[512,128]{1,0:T(8,128)S(1)}, f32[512,128]{1,0:T(8,128)}) fusion(f32[512,512]{1,0:T(8,128)} %get-tuple-element.15, s32[]{:T(128)S(6)} %select_n.2, f32[512,512]{1,0:T(8,128)S(1)} %get-tuple-element.12), kind=kLoop, calls=%fused_computation.11 | loop fusion | flops 131072 | bytes 1048580 | tf_op jit(solution)/shard_map/mul | solution.py:474
  113.5 2.0 %fusion.10 = (f32[128,512]{1,0:T(8,128)S(1)}, f32[128,512]{1,0:T(8,128)}, f32[128,512]{1,0:T(8,128)}, f32[128,512]{1,0:T(8,128)S(1)}) fusion(f32[128,1024]{1,0:T(8,128)} %copy-done.6), kind=kLoop, calls=%fused_computation.18 | loop fusion | flops 131072 | bytes 1572864 | tf_op jit(solution)/shard_map/slice | solution.py:462
  115.4 0.1 stack_reshape.6
  115.5 1.0 copy.6
  116.5 0.1 stack_reshape.7
  116.6 0.3 copy.7
  116.9 1.6 pad_maximum_fusion
  118.5 0.4 reshape.23
  119.0 0.0 copy-start.5
  119.0 8.1 %shard_map.60 = f32[4,128,256]{2,1,0:T(8,128)S(1)} custom-call(f32[4,128,256]{2,1,0:T(8,128)S(1)} %bitcast.16), custom_call_target="tpu_custom_call" | custom-call | tf_op jit(solution)/shard_map/pallas_call | solution.py:278
  127.1 2.3 %convolution_add_fusion = f32[512,256]{1,0:T(8,128)S(1)} fusion(f32[512,256]{1,0:T(8,128)S(1)} %bitcast.14, f32[512,1024]{1,0:T(8,128)} %copy-done.1, f32[512,128]{1,0:T(8,128)S(1)} %get-tuple-element.23, f32[512,128]{1,0:T(8,128)} %get-tuple-element.24), kind=kOutput, calls=%fused_computation | convolution fusion | flops 402915328 | bytes 2621440 | tf_op jit(solution)/shard_map/dot_general | solution.py:18
  129.4 0.0 copy-done.5
  129.4 0.0 copy-start.2
  129.4 1.0 fusion.11
  130.5 0.5 copy-done.2
  131.0 1.9 %convolution_add_fusion.1 = f32[512,128]{1,0:T(8,128)S(1)} fusion(f32[512,1024]{1,0:T(8,128)S(1)} %copy-done.2, f32[512,256]{1,0:T(8,128)S(1)} %bitcast.15, f32[512,512]{1,0:T(8,128)} %get-tuple-element.16, s32[]{:T(128)S(6)} %select_n.2), kind=kOutput, calls=%fused_computation.1 | convolution fusion | flops 201457664 | bytes 1835012 | tf_op jit(solution)/shard_map/dot_general | solution.py:18
  133.0 1.8 %fusion.2 = f32[512,128]{1,0:T(8,128)S(1)} fusion(f32[1024,512]{1,0:T(8,128)S(1)} %get-tuple-element.14, f32[512,128]{1,0:T(8,128)S(1)} %convolution_add_fusion.1, f32[512,128]{1,0:T(8,128)S(1)} %slice.42), kind=kOutput, calls=%fused_computation.6 | convolution fusion | flops 402784256 | bytes 2883584 | tf_op jit(solution)/shard_map/dot_general | solution.py:18
  134.8 0.1 maximum_bitcast_fusion.x_ref
  134.8 37.6 %shard_map.61 = f32[3,64,128]{2,1,0:T(8,128)S(1)} custom-call(f32[8,3,64,128]{3,2,1,0:T(8,128)S(1)} %maximum_bitcast_fusion.x_ref), custom_call_target="tpu_custom_call" | custom-call | tf_op jit(solution)/shard_map/pallas_call | solution.py:278
  172.5 0.6 copy.9
  (2 shorter events, 0.1 us)
Async XLA Ops:
  0.6 1.0 copy-start.7
  1.7 1.0 copy-start.8
  64.2 1.7 copy-start
  65.9 1.4 copy-start.1
  67.3 1.6 copy-start.3
  109.9 1.7 copy-start.6
  110.0 1.8 %copy-start.4 = (f32[512,512]{1,0:T(8,128)}, f32[512,512]{1,0:T(8,128)S(1)}, u32[]{:S(2)}) copy-start(f32[512,512]{1,0:T(8,128)S(1)} %get-tuple-element.12) | copy-start | bytes 3145732
  119.0 10.4 %copy-start.5 = (f32[512,512]{1,0:T(8,128)S(1)}, f32[512,512]{1,0:T(8,128)}, u32[]{:S(2)}) copy-start(f32[512,512]{1,0:T(8,128)} %copy-done.4) | copy-start | bytes 3145732
  129.4 1.6 copy-start.2

commit v3 on v2

--- a/solution.py
+++ b/solution.py
@@ -129,8 +129,6 @@
                  g * group + (j + k) % group, c)
 
     own_win = w_ref.at[:, :, lanes(parity)]
-    send(has_right, own_win, win_at(g, j, parity), wzsend.at[0, g], wzrecv.at[g], r + group, c)
-    send(has_left, own_win, win_at(g, j, parity), wzsend.at[1, g], wzrecv.at[g], r - group, c)
     spread_win(None, own_win, g)
     win_ref[:, pl.ds(pl.multiple_of(r * tall, tall), tall), :] = w_ref[...]
     for step in range(1, cols):
@@ -150,30 +148,37 @@
                 to = (c + k) % cols if k else mate
                 send(None, p_ref, slot(own_ref, c), osend.at[k], orecv.at[c], r, to)
             slot(own_ref, c)[...] = p_ref[...]
-        for side in range(2):
-            gs = g - step if side == 0 else g + step
-            there = gs >= 0 if side == 0 else gs < cols
-            onward = jnp.logical_and(there, has_right if side == 0 else has_left)
-            gs = jnp.clip(gs, 0, cols - 1)
-            block = win_at(gs, j, parity)
-            pl.when(there)(functools.partial(await_recv, block, wzrecv.at[gs]))
-            send(onward, block, block, wzsend.at[side, gs], wzrecv.at[gs],
-                 r + group if side == 0 else r - group, c)
-            spread_win(there, block, gs)
-            send(there, block, block, wdsend.at[j, gs], wdrecv.at[j, gs], r, mate)
-        relay_x(step - 1)
+        if step < cols - 1:
+            relay_x(step - 1)
+    for k in range(group):
+        jj = (j + k) % group
+        block = win_at(g, jj, parity)
+        if k:
+            await_recv(block, wxrecv.at[jj, g])
+            send(None, block, block, wdsend.at[jj, g], wdrecv.at[jj, g], r, mate)
+        first = block if k else own_win
+        send(has_right, first, block, wzsend.at[0, jj, g], wzrecv.at[jj, g], r + group, c)
+        send(has_left, first, block, wzsend.at[1, jj, g], wzrecv.at[jj, g], r - group, c)
+    relay_x(cols - 2)
     relay_x(cols - 1)
+    for step in range(1, cols):
+        for k in range(group):
+            jj = (j + k) % group
+            for side in range(2):
+                gs = g - step if side == 0 else g + step
+                there = gs >= 0 if side == 0 else gs < cols
+                onward = jnp.logical_and(there, has_right if side == 0 else has_left)
+                gs = jnp.clip(gs, 0, cols - 1)
+                block = win_at(gs, jj, parity)
+                pl.when(there)(functools.partial(await_recv, block, wzrecv.at[jj, gs]))
+                send(onward, block, block, wzsend.at[side, jj, gs], wzrecv.at[jj, gs],
+                     r + group if side == 0 else r - group, c)
+                send(there, block, block, wdsend.at[jj, gs], wdrecv.at[jj, gs], r, mate)
     for k in range(2, cols, 2):
         column = (c + k) % cols
         block = slot(own_ref, column)
         await_recv(block, orecv.at[column])
         send(None, block, block, ofwd.at[column], orecv.at[column], r, mate)
-    for k in range(1, group):
-        jj = (j + k) % group
-        for gg in range(cols):
-            block = win_at(gg, jj, parity)
-            await_recv(block, wxrecv.at[jj, gg])
-            send(None, block, block, wdsend.at[jj, gg], wdrecv.at[jj, gg], r, mate)
     for k in range(0, cols, 2):
         column = (mate + k) % cols
         await_recv(slot(own_ref, column), orecv.at[column])
@@ -224,8 +229,8 @@
             dma((cols,)),
             dma((cols,)),
             dma((cols,)),
-            dma((2, cols)),
-            dma((cols,)),
+            dma((2, group, cols)),
+            dma((group, cols)),
             dma((group, cols)),
             dma((group, cols)),
             dma((group, cols)),

time: 174 us -> 159 us (0.914)
  Pallas kernels: 148 us -> 134 us
    pallas_call x1, Pallas kernels: 41 us -> 29.9 us  [images_and_inverses(): pl.pallas_call(functools.partial(images_kernel, cols), out_shape=(jax.Sha...]
    pallas_call x2, Pallas kernels: 45.8 us -> 41.1 us  [exchange(): pl.pallas_call(functools.partial(exchange_kernel, axis, total, add), out_...]
where the time goes in v3:
time: 159 us
  Pallas kernels  134 us (84%)
  local copies, waits for them, and re-layouts  11.6 us (7%)
  matrix products  7.02 us (4%)
  other arithmetic  5.39 us (3%)
    pallas_call x1, Pallas kernels, gather_all(): pl.pallas_call(functools.partial(gather_kernel, cols, group, halves), out...  63 us
    pallas_call x2, Pallas kernels, exchange(): pl.pallas_call(functools.partial(exchange_kernel, axis, total, add), out_...  41.1 us
    pallas_call x1, Pallas kernels, images_and_inverses(): pl.pallas_call(functools.partial(images_kernel, cols), out_shape=(jax.Sha...  29.9 us
    unnamed x19, local copies, waits for them, and re-layouts  8.01 us
    dot_general x4, matrix products, dot(): lax.dot_general(left, right, (dims, ((), ())), precision=precision, prefe...  7.02 us

profile of v3, /device:TPU:11, one launch (start us, length us, event | category | flops | bytes accessed | tf_op | source)
XLA Modules:
  0.0 158.7 jit_solution(16534897666551094500)
XLA Ops:
  0.6 0.0 copy-start.7
  0.6 1.0 copy-done.7
  1.7 0.0 copy-start.8
  1.7 1.0 copy-done.8
  2.7 63.0 %shard_map.58 = (f32[2,512,1024]{2,1,0:T(8,128)}, f32[512,1024]{1,0:T(8,128)S(1)}, f32[3,512,512]{2,1,0:T(8,128)S(1)}) custom-call(f32[512,256]{1,0:T(8,128)S(1)} %copy-done.7, f32[3,64,512]{2,1,0:T(8,128)S(1)} %copy-done.8), custom_call_target="tpu_custom_call" | custom-call | tf_op jit(solution)/shard_map/pallas_call | solution.py:212
  65.7 0.0 copy-start
  65.7 1.7 %copy-done = f32[3,512,512]{2,1,0:T(8,128)} copy-done((f32[3,512,512]{2,1,0:T(8,128)}, f32[3,512,512]{2,1,0:T(8,128)S(1)}, u32[]{:S(2)}) %copy-start) | copy-done | bytes 3145752
  67.3 0.0 copy-start.1
  67.4 1.4 copy-done.1
  68.8 0.0 copy-start.3
  68.8 1.6 %copy-done.3 = f32[512,1024]{1,0:T(8,128)S(1)} copy-done((f32[512,1024]{1,0:T(8,128)S(1)}, f32[512,1024]{1,0:T(8,128)}, u32[]{:S(2)}) %copy-start.3) | copy-done | bytes 2097176
  70.3 29.9 %shard_map.59 = (f32[128,1024]{1,0:T(8,128)S(1)}, f32[512,512]{1,0:T(8,128)S(1)}, f32[1024,512]{1,0:T(8,128)S(1)}) custom-call(f32[512,1024]{1,0:T(8,128)S(1)} %copy-done.3, f32[1024,1024]{1,0:T(8,128)} %bitcast.17, f32[3,512,512]{2,1,0:T(8,128)} %copy-done), custom_call_target="tpu_custom_call" | custom-call | tf_op jit(solution)/shard_map/pallas_call | solution.py:436
  100.2 0.0 copy-start.6
  100.2 0.0 copy-start.4
  100.2 1.6 %fusion.8 = (f32[512,512]{1,0:T(8,128)}, f32[512,512]{1,0:T(8,128)}) fusion(f32[1024,512]{1,0:T(8,128)S(1)} %get-tuple-element.14), kind=kLoop, calls=%fused_computation.16 | loop fusion | bytes 4194304 | tf_op jit(solution)/shard_map/slice | solution.py:465
  101.9 0.0 copy-done.6
  101.9 0.1 copy-done.4
  102.0 1.7 %dynamic-slice_multiply_fusion = (f32[512,128]{1,0:T(8,128)S(1)}, f32[512,128]{1,0:T(8,128)}) fusion(f32[512,512]{1,0:T(8,128)} %get-tuple-element.15, s32[]{:T(128)S(6)} %select_n.2, f32[512,512]{1,0:T(8,128)S(1)} %get-tuple-element.12), kind=kLoop, calls=%fused_computation.11 | loop fusion | flops 131072 | bytes 1048580 | tf_op jit(solution)/shard_map/mul | solution.py:479
  103.8 2.0 %fusion.10 = (f32[128,512]{1,0:T(8,128)S(1)}, f32[128,512]{1,0:T(8,128)}, f32[128,512]{1,0:T(8,128)}, f32[128,512]{1,0:T(8,128)S(1)}) fusion(f32[128,1024]{1,0:T(8,128)} %copy-done.6), kind=kLoop, calls=%fused_computation.18 | loop fusion | flops 131072 | bytes 1572864 | tf_op jit(solution)/shard_map/slice | solution.py:467
  105.7 0.1 stack_reshape.6
  105.8 1.0 copy.6
  106.8 0.1 stack_reshape.7
  106.9 0.3 copy.7
  107.2 1.6 %pad_maximum_fusion = f32[128,4,2,128]{3,2,0,1:T(2,128)S(1)} fusion(f32[128,4,1,128]{3,2,0,1:T(1,128)S(1)} %copy.7, f32[128,4,1,128]{3,2,0,1:T(1,128)} %copy.6), kind=kLoop, calls=%fused_computation.5 | loop fusion | flops 131072 | bytes 1048576 | tf_op jit(solution)/shard_map/stack | solution.py:471
  108.8 0.4 reshape.23
  109.2 0.0 copy-start.5
  109.2 8.1 %shard_map.60 = f32[4,128,256]{2,1,0:T(8,128)S(1)} custom-call(f32[4,128,256]{2,1,0:T(8,128)S(1)} %bitcast.16), custom_call_target="tpu_custom_call" | custom-call | tf_op jit(solution)/shard_map/pallas_call | solution.py:283
  117.4 2.3 %convolution_add_fusion = f32[512,256]{1,0:T(8,128)S(1)} fusion(f32[512,256]{1,0:T(8,128)S(1)} %bitcast.14, f32[512,1024]{1,0:T(8,128)} %copy-done.1, f32[512,128]{1,0:T(8,128)S(1)} %get-tuple-element.23, f32[512,128]{1,0:T(8,128)} %get-tuple-element.24), kind=kOutput, calls=%fused_computation | convolution fusion | flops 402915328 | bytes 2621440 | tf_op jit(solution)/shard_map/dot_general | solution.py:18
  119.7 0.0 copy-done.5
  119.7 0.0 copy-start.2
  119.7 1.0 fusion.11
  120.8 0.5 copy-done.2
  121.3 1.9 %convolution_add_fusion.1 = f32[512,128]{1,0:T(8,128)S(1)} fusion(f32[512,1024]{1,0:T(8,128)S(1)} %copy-done.2, f32[512,256]{1,0:T(8,128)S(1)} %bitcast.15, f32[512,512]{1,0:T(8,128)} %get-tuple-element.16, s32[]{:T(128)S(6)} %select_n.2), kind=kOutput, calls=%fused_computation.1 | convolution fusion | flops 201457664 | bytes 1835012 | tf_op jit(solution)/shard_map/dot_general | solution.py:18
  123.2 1.8 %fusion.2 = f32[512,128]{1,0:T(8,128)S(1)} fusion(f32[1024,512]{1,0:T(8,128)S(1)} %get-tuple-element.14, f32[512,128]{1,0:T(8,128)S(1)} %convolution_add_fusion.1, f32[512,128]{1,0:T(8,128)S(1)} %slice.42), kind=kOutput, calls=%fused_computation.6 | convolution fusion | flops 402784256 | bytes 2883584 | tf_op jit(solution)/shard_map/dot_general | solution.py:18
  125.0 0.1 maximum_bitcast_fusion.x_ref
  125.1 33.0 %shard_map.61 = f32[3,64,128]{2,1,0:T(8,128)S(1)} custom-call(f32[8,3,64,128]{3,2,1,0:T(8,128)S(1)} %maximum_bitcast_fusion.x_ref), custom_call_target="tpu_custom_call" | custom-call | tf_op jit(solution)/shard_map/pallas_call | solution.py:283
  158.1 0.6 copy.9
  (2 shorter events, 0.1 us)
Async XLA Ops:
  0.6 1.0 copy-start.7
  1.7 1.0 copy-start.8
  65.7 1.7 %copy-start = (f32[3,512,512]{2,1,0:T(8,128)}, f32[3,512,512]{2,1,0:T(8,128)S(1)}, u32[]{:S(2)}) copy-start(f32[3,512,512]{2,1,0:T(8,128)S(1)} %get-tuple-element.10.win_ref) | copy-start | bytes 9437188
  67.3 1.4 copy-start.1
  68.8 1.6 %copy-start.3 = (f32[512,1024]{1,0:T(8,128)S(1)}, f32[512,1024]{1,0:T(8,128)}, u32[]{:S(2)}) copy-start(f32[512,1024]{1,0:T(8,128)} %z_ref.1) | copy-start | bytes 6291460
  100.2 1.7 %copy-start.6 = (f32[128,1024]{1,0:T(8,128)}, f32[128,1024]{1,0:T(8,128)S(1)}, u32[]{:S(2)}) copy-start(f32[128,1024]{1,0:T(8,128)S(1)} %get-tuple-element.11) | copy-start | bytes 1572868
  100.2 1.8 %copy-start.4 = (f32[512,512]{1,0:T(8,128)}, f32[512,512]{1,0:T(8,128)S(1)}, u32[]{:S(2)}) copy-start(f32[512,512]{1,0:T(8,128)S(1)} %get-tuple-element.12) | copy-start | bytes 3145732
  109.2 10.4 %copy-start.5 = (f32[512,512]{1,0:T(8,128)S(1)}, f32[512,512]{1,0:T(8,128)}, u32[]{:S(2)}) copy-start(f32[512,512]{1,0:T(8,128)} %copy-done.4) | copy-start | bytes 3145732
  119.7 1.6 %copy-start.2 = (f32[512,1024]{1,0:T(8,128)S(1)}, f32[512,1024]{1,0:T(8,128)}, u32[]{:S(2)}) copy-start(f32[512,1024]{1,0:T(8,128)} %copy-done.1) | copy-start | bytes 6291460
